TPU v7x, 32 devices: a whole 2x2x4 slice. The times are simulated.
32 devices in a mesh: ka: 4 (over y, core), op: 4 (over z), row: 2 (over x).
Axes of the slice: x: 2, y: 2, z: 4, core: 2. Of those that a mesh axis runs over, the one named last changes fastest.
Arguments:
- kgrid: int32 [3, 256], P(None, ('ka', 'op', 'row')), may hold values from 0 to 63
- rvec: int32 [3, 256], replicated, may hold values from -8 to 8
- degen: int32 [256], replicated, may hold values from 1 to 4
- operators: bfloat16 [4, 256, 12800], P('op', ('ka', 'row')), may hold values from -1 to 1
- vectors: bfloat16 [256, 12800], P(('ka', 'op', 'row')), may hold values from -0.5 to 0.5
Outputs:
- density: float32 [3, 256], P(None, ('ka', 'op', 'row'))
- magnetization: float32 [3], replicated
All inputs are finite; a program needn't handle non-finite values.
Results may differ from a plain program's by a relative error of at most 0.012.
Values may be sent and summed in bfloat16 or wider, within the bound.
No kernel may reach another device: no remote copies, remote signals or barrier semaphores. Data moves between devices by JAX's collectives and lax.ppermute only.
A program may use at most 64 MiB of HBM per device.

v0:
```python
import math
import jax
import jax.numpy as jnp
from jax import lax
from jax.sharding import PartitionSpec as P

W = 80
GRID = 64
SMEARING = 0.5


def phase_pair(points, lattice, weights):
    winding = (
        points[0][:, None] * lattice[0][None, :]
        + points[1][:, None] * lattice[1][None, :]
        + points[2][:, None] * lattice[2][None, :]
    )
    winding = jnp.mod(winding, GRID)
    angle = 2.0 * math.pi / GRID * winding.astype(jnp.float32)
    inverse = 1.0 / weights.astype(jnp.float32)
    cosine = (jnp.cos(angle) * inverse[None, :]).astype(jnp.bfloat16)
    sine = (jnp.sin(angle) * inverse[None, :]).astype(jnp.bfloat16)
    return (cosine, sine)


def mix_table(table, block):
    return jnp.einsum("kr,nrx->nkx", table, block, preferred_element_type=jnp.float32)


def make_fold(points, lattice, weights):

    def accumulate(carry, piece, start):
        cosine, sine = phase_pair(points, lattice, weights)
        half = piece.shape[2] // 2
        real_in = piece[:, :, :half]
        imag_in = piece[:, :, half:]
        real_out = mix_table(cosine, real_in) - mix_table(sine, imag_in)
        imag_out = mix_table(cosine, imag_in) + mix_table(sine, real_in)
        return jnp.concatenate([real_out, imag_out], axis=1)

    return accumulate


def density_terms(rot_real, rot_imag):
    ham_real = rot_real[0]
    ham_imag = rot_imag[0]
    conn_real = rot_real[1:]
    conn_imag = rot_imag[1:]
    levels = jnp.diagonal(ham_real, axis1=1, axis2=2).astype(jnp.float32)
    filled = jax.nn.sigmoid(-levels / SMEARING)
    vacant = 1.0 - filled

    def multiply(left, right):
        return jnp.einsum("knm,bkml->bknl", left, right, preferred_element_type=jnp.float32)

    prod_real = multiply(ham_real, conn_real) - multiply(ham_imag, conn_imag)
    prod_imag = multiply(ham_real, conn_imag) + multiply(ham_imag, conn_real)
    weight = filled[None, :, :, None] * vacant[None, :, None, :]
    left_real = conn_real.astype(jnp.float32) * weight
    left_imag = conn_imag.astype(jnp.float32) * weight
    traces = jnp.einsum(
        "aknm,bkmn->abk", left_real, prod_imag, precision=lax.Precision.HIGHEST
    ) + jnp.einsum("aknm,bkmn->abk", left_imag, prod_real, precision=lax.Precision.HIGHEST)
    density = jnp.stack(
        [traces[1, 2] - traces[2, 1], traces[2, 0] - traces[0, 2], traces[0, 1] - traces[1, 0]]
    )
    return density / W


def per_device(kgrid, rvec, degen, operators, vectors):
    own = kgrid.shape[1]
    entries = vectors.shape[1] // 2
    count_ka = lax.axis_size("ka")
    count_op = lax.axis_size("op")
    count_row = lax.axis_size("row")
    count_all = own * count_ka * count_op * count_row
    points = lax.all_gather(kgrid, "op", axis=1, tiled=True)
    folder = make_fold(points, rvec, degen)
    points_count = points.shape[1]
    zeroed = jnp.zeros((1, 2 * points_count, entries), jnp.float32)
    summed = folder(
        zeroed, lax.all_gather(operators, ("ka", "row"), axis=1, tiled=True), jnp.int32(0)
    )
    real_k = summed[:, :points_count].astype(jnp.bfloat16)
    imag_k = summed[:, points_count:].astype(jnp.bfloat16)
    real_k, imag_k = (
        lax.all_to_all(real_k, "op", split_axis=1, concat_axis=0, tiled=True),
        lax.all_to_all(imag_k, "op", split_axis=1, concat_axis=0, tiled=True),
    )
    halves = vectors.reshape(own, 2, W, W)
    vec_real = halves[:, 0]
    vec_imag = halves[:, 1]

    def apply_right(left, right):
        return jnp.einsum("kij,kjn->kin", left, right, preferred_element_type=jnp.float32)

    def apply_left(left, right):
        return jnp.einsum("kin,kim->knm", left, right, preferred_element_type=jnp.float32)

    def rotate(block):
        op_real, op_imag = block
        prod_real = (apply_right(op_real, vec_real) - apply_right(op_imag, vec_imag)).astype(
            jnp.bfloat16
        )
        prod_imag = (apply_right(op_real, vec_imag) + apply_right(op_imag, vec_real)).astype(
            jnp.bfloat16
        )
        rot_real = (apply_left(vec_real, prod_real) + apply_left(vec_imag, prod_imag)).astype(
            jnp.bfloat16
        )
        rot_imag = (apply_left(vec_real, prod_imag) - apply_left(vec_imag, prod_real)).astype(
            jnp.bfloat16
        )
        return (rot_real, rot_imag)

    rot_real, rot_imag = lax.map(
        rotate, (real_k.reshape(4, own, W, W), imag_k.reshape(4, own, W, W))
    )
    density = density_terms(rot_real, rot_imag)
    magnetization = lax.psum(jnp.sum(density, axis=1), ("ka", "op", "row")) / count_all
    return (density, magnetization)


def solution(mesh):
    in_specs = (
        P(None, ("ka", "op", "row")),
        P(),
        P(),
        P("op", ("ka", "row"), None),
        P(("ka", "op", "row"), None),
    )
    out_specs = (P(None, ("ka", "op", "row")), P())
    return jax.shard_map(
        per_device, mesh=mesh, in_specs=in_specs, out_specs=out_specs, check_vma=False
    )
```

profile of v0, /device:TPU:10, one launch (start us, length us, event | category | flops | bytes accessed | tf_op | source)
XLA Modules:
  0.0 192.2 jit_solution(1296548206554515161)
XLA Ops:
  7.9 12.3 %all-gather = s32[4,8,3]{1,2,0:T(4,128)S(1)} all-gather(s32[1,8,3]{1,2,0:T(4,128)} %bitcast.177), channel_id=1, replica_groups=mesh['ka'=4,'op'=4,'row'=2] {'op'}, dimensions={0}, use_global_device_ids=true | all-gather | bytes 480 | tf_op jit(solution)/shard_map/all_gather | solution.py:77
  21.0 0.8 fusion.79
  21.8 35.7 %all-gather.3.cloned.1.call-done = bf16[1,256,12800]{2,1,0:T(8,128)(2,1)} async-done(((bf16[1,32,12800]{2,1,0:T(8,128)(2,1)}), bf16[1,256,12800]{2,1,0:T(8,128)(2,1)}) %all-gather.3.cloned.1.call-update) | async-done | bytes 6553616 | tf_op jit(solution)/shard_map/all_gather | solution.py:82
  57.5 2.8 %fusion.26 = f32[32,6400]{1,0:T(8,128)S(1)} fusion(bf16[1,256,12800]{2,1,0:T(8,128)(2,1)} %all-gather.3.cloned.1.call-done, f32[256]{0:T(256)S(1)} %convert_divide_fusion, s32[256]{0:T(256)S(1)} %bitcast.168, s32[32]{0:T(128)S(1)} %get-tuple-element.69, s32[256]{0:T(256)S(1)} %bitcast.172, s32[32]{0:T(128)S(1)} %get-tuple-element.70, s32[256]{0:T(256)S(1)} %bitcast.164, ...), kind=kOutput, calls=%fused_computation.35 | convolution fusion | flops 105021440 | bytes 4100480 | tf_op jit(solution)/shard_map/kr,nrx->nkx/dot_general | solution.py:27
  60.3 2.8 %fusion.25 = bf16[1,32,6400]{2,1,0:T(8,128)(2,1)S(1)} fusion(f32[32,6400]{1,0:T(8,128)S(1)} %fusion.26, bf16[1,256,12800]{2,1,0:T(8,128)(2,1)} %all-gather.3.cloned.1.call-done, f32[256]{0:T(256)S(1)} %convert_divide_fusion, s32[256]{0:T(256)S(1)} %bitcast.169, s32[32]{0:T(128)S(1)} %get-tuple-element.69, s32[256]{0:T(256)S(1)} %bitcast.173, ...), kind=kOutput, calls=%fused_computation.32 | convolution fusion | flops 105431040 | bytes 4510080 | tf_op jit(solution)/shard_map/kr,nrx->nkx/dot_general | solution.py:27
  64.2 3.1 %reduce.10 = bf16[32,6400]{1,0:T(8,128)(2,1)S(1)} reduce(bf16[32,1,6400]{2,1,0:T(2,128)(2,1)S(1)} %bitcast.162, bf16[]{:T(256)} %broadcast.118), dimensions={1}, to_apply=%bitcast.125.reduce_sub_computation | reduce | bytes 819202
  67.3 0.9 reshape.142
  68.2 5.1 %all-to-all-start = ((bf16[4,2,25600]{2,1,0:T(2,128)(2,1)}), bf16[4,2,25600]{2,1,0:T(2,128)(2,1)S(1)}, u32[]{:S(2)}, u32[]{:S(2)}) async-start(bf16[4,2,25600]{2,1,0:T(2,128)(2,1)} %reshape.142), calls=%async_computation | async-start | bytes 819200 | tf_op jit(solution)/shard_map/all_to_all | solution.py:87
  73.3 2.8 %fusion.27 = f32[32,6400]{1,0:T(8,128)S(1)} fusion(bf16[1,256,12800]{2,1,0:T(8,128)(2,1)} %all-gather.3.cloned.1.call-done, f32[256]{0:T(256)S(1)} %convert_divide_fusion, s32[256]{0:T(256)S(1)} %bitcast.170, s32[32]{0:T(128)S(1)} %get-tuple-element.69, s32[256]{0:T(256)S(1)} %bitcast.174, s32[32]{0:T(128)S(1)} %get-tuple-element.70, s32[256]{0:T(256)S(1)} %bitcast.166, ...), kind=kOutput, calls=%fused_computation.36 | convolution fusion | flops 105021440 | bytes 4100480 | tf_op jit(solution)/shard_map/kr,nrx->nkx/dot_general | solution.py:27
  76.1 2.8 %fusion.24 = bf16[1,32,6400]{2,1,0:T(8,128)(2,1)S(1)} fusion(f32[32,6400]{1,0:T(8,128)S(1)} %fusion.27, bf16[1,256,12800]{2,1,0:T(8,128)(2,1)} %all-gather.3.cloned.1.call-done, f32[256]{0:T(256)S(1)} %convert_divide_fusion, s32[256]{0:T(256)S(1)} %bitcast.171, s32[32]{0:T(128)S(1)} %get-tuple-element.69, s32[256]{0:T(256)S(1)} %bitcast.175, ...), kind=kOutput, calls=%fused_computation.31 | convolution fusion | flops 105431040 | bytes 4510080 | tf_op jit(solution)/shard_map/kr,nrx->nkx/dot_general | solution.py:27
  79.6 3.1 %reduce.11 = bf16[32,6400]{1,0:T(8,128)(2,1)S(1)} reduce(bf16[32,1,6400]{2,1,0:T(2,128)(2,1)S(1)} %bitcast.163, bf16[]{:T(256)} %broadcast.118), dimensions={1}, to_apply=%bitcast.124.reduce_sub_computation | reduce | bytes 819202
  82.7 0.9 reshape.144
  83.5 5.7 %all-to-all-start.1 = ((bf16[4,2,25600]{2,1,0:T(2,128)(2,1)}), bf16[4,2,25600]{2,1,0:T(2,128)(2,1)S(1)}, u32[]{:S(2)}, u32[]{:S(2)}) async-start(bf16[4,2,25600]{2,1,0:T(2,128)(2,1)} %reshape.144), calls=%async_computation.1 | async-start | bytes 819200 | tf_op jit(solution)/shard_map/all_to_all | solution.py:88
  90.1 2.3 %bitcast_reduce_fusion.1 = bf16[32,6400]{1,0:T(8,128)(2,1)S(1)} fusion(bf16[32,1,6400]{2,1,0:T(2,128)(2,1)S(1)} %reshape.143), kind=kLoop, calls=%fused_computation.108 | loop fusion | bytes 819200 | tf_op jit(solution)/shard_map/all_to_all | solution.py:87
  92.3 1.1 reshape.122
  93.4 4.8 %all-to-all-done.1 = bf16[4,2,25600]{2,1,0:T(2,128)(2,1)S(1)} async-done(((bf16[4,2,25600]{2,1,0:T(2,128)(2,1)}), bf16[4,2,25600]{2,1,0:T(2,128)(2,1)S(1)}, u32[]{:S(2)}, u32[]{:S(2)}) %all-to-all-start.1) | async-done | bytes 409632 | tf_op jit(solution)/shard_map/all_to_all | solution.py:88
  98.6 2.3 %bitcast_reduce_fusion = bf16[32,6400]{1,0:T(8,128)(2,1)S(1)} fusion(bf16[32,1,6400]{2,1,0:T(2,128)(2,1)S(1)} %reshape.145), kind=kLoop, calls=%fused_computation.107 | loop fusion | bytes 819200 | tf_op jit(solution)/shard_map/all_to_all | solution.py:88
  100.9 1.1 reshape.124
  102.0 7.9 %while.12 = (s32[]{:T(128)}, bf16[4,8,80,80]{2,3,1,0:T(8,128)(2,1)S(1)}, bf16[4,8,80,80]{2,3,1,0:T(8,128)(2,1)S(1)}, bf16[4,8,80,80]{3,2,1,0:T(8,128)(2,1)S(1)},...) while((s32[]{:T(128)}, ...), condition=%wide.region_1.2_spmd, body=%wide.region_0.1_spmd.sunk | while | flops 65945600 | bytes 5038189 | solution.py:116
  110.5 1.6 copy.74
  112.1 3.7 %gather_fusion = bf16[80,8]{1,0:T(8,128)(2,1)S(1)} fusion(bf16[8,80,80]{0,2,1:T(8,128)(2,1)} %copy.74, s32[80]{0:T(128)S(1)} %or_bitcast_fusion), kind=kCustom, calls=%fused_computation | custom fusion | bytes 3200 | tf_op jit(solution)/shard_map/jit(diagonal)/gather | solution.py:49
  115.9 1.1 copy.73
  117.0 1.2 fusion.48
  118.2 2.2 %fusion.28 = f32[3,8,80,80]{2,3,0,1:T(8,128)} fusion(f32[8,3,80,80]{3,2,1,0:T(8,128)S(1)} %fusion.46, bf16[4,8,80,80]{3,2,1,0:T(8,128)(2,1)} %copy.73, bf16[4,8,80,80]{2,3,1,0:T(8,128)(2,1)S(1)} %get-tuple-element.40), kind=kOutput, calls=%fused_computation.38 | convolution fusion | flops 24729600 | bytes 1802240 | tf_op jit(solution)/shard_map/knm,bkml->bknl/dot_general | solution.py:54
  120.4 2.4 %copy.78 = f32[3,8,80,80]{3,0,2,1:T(4,128)} copy(f32[3,8,80,80]{2,3,0,1:T(8,128)} %fusion.28) | data formatting | bytes 1228800 | tf_op jit(solution)/shard_map/sub | solution.py:56
  122.9 1.1 convert_multiply_fusion
  124.1 2.1 %fusion.29 = f32[3,8,80,80]{2,3,0,1:T(8,128)} fusion(f32[8,3,80,80]{3,2,1,0:T(8,128)S(1)} %fusion.48, bf16[4,8,80,80]{3,2,1,0:T(8,128)(2,1)} %copy.73, bf16[4,8,80,80]{2,3,1,0:T(8,128)(2,1)S(1)} %get-tuple-element.41), kind=kOutput, calls=%fused_computation.40 | convolution fusion | flops 24729600 | bytes 1802240 | tf_op jit(solution)/shard_map/knm,bkml->bknl/dot_general | solution.py:54
  126.2 2.4 %copy.76 = f32[3,8,80,80]{3,0,2,1:T(4,128)} copy(f32[3,8,80,80]{2,3,0,1:T(8,128)} %fusion.29) | data formatting | bytes 1228800 | tf_op jit(solution)/shard_map/add | solution.py:57
  128.7 7.4 %fusion.34 = f32[8,3,3]{2,1,0:T(4,128)S(1)} fusion(f32[3,8,80,80]{3,0,2,1:T(4,128)} %copy.76, f32[3,8,80,80]{2,3,0,1:T(8,128)S(1)} %get-tuple-element.62), kind=kOutput, calls=%fused_computation.45 | convolution fusion | flops 5529600 | bytes 1229088 | tf_op jit(solution)/shard_map/aknm,bkmn->abk/dot_general | solution.py:61
  136.0 6.8 %fusion.43 = f32[3,3,8]{0,1,2:T(4,128)S(1)} fusion(f32[8,3,3]{2,1,0:T(4,128)S(1)} %fusion.34, f32[3,8,80,80]{3,0,2,1:T(4,128)} %copy.78, f32[3,8,80,80]{2,3,0,1:T(8,128)S(1)} %copy-done), kind=kOutput, calls=%fused_computation.48 | convolution fusion | flops 5529672 | bytes 1229376 | tf_op jit(solution)/shard_map/aknm,bkmn->abk/dot_general | solution.py:63
  143.0 0.7 fusion.78
  143.7 41.1 %psum.7 = f32[3]{0:T(128)S(1)} all-reduce(f32[3]{0:T(128)S(1)} %get-tuple-element.59), channel_id=1, replica_groups=mesh['ka'=4,'op'=4,'row'=2] {'ka','op','row'}, use_global_device_ids=true, to_apply=%region_3.4 | all-reduce | flops 3 | bytes 24 | tf_op jit(solution)/shard_map/psum | solution.py:120
  (64 shorter events, 13.6 us)
Async XLA Ops:
  7.2 50.4 %all-gather.3.cloned.1.call-start = ((), (), s32[]{:S(2)}) async-start(), calls=%async_computation.2 | async-start | bytes 7372800 | tf_op jit(solution)/shard_map/all_gather | solution.py:82
  68.2 15.3 %all-to-all-start = ((bf16[4,2,25600]{2,1,0:T(2,128)(2,1)}), bf16[4,2,25600]{2,1,0:T(2,128)(2,1)S(1)}, u32[]{:S(2)}, u32[]{:S(2)}) async-start(bf16[4,2,25600]{2,1,0:T(2,128)(2,1)} %reshape.142), calls=%async_computation | async-start | bytes 819200 | tf_op jit(solution)/shard_map/all_to_all | solution.py:87
  76.1 13.1 %copy-start.2 = (bf16[8,12800]{1,0:T(8,128)(2,1)S(1)}, bf16[8,12800]{1,0:T(8,128)(2,1)}, u32[]{:S(2)}) copy-start(bf16[8,12800]{1,0:T(8,128)(2,1)} %param.11) | copy-start | bytes 614404
  83.5 14.7 %all-to-all-start.1 = ((bf16[4,2,25600]{2,1,0:T(2,128)(2,1)}), bf16[4,2,25600]{2,1,0:T(2,128)(2,1)S(1)}, u32[]{:S(2)}, u32[]{:S(2)}) async-start(bf16[4,2,25600]{2,1,0:T(2,128)(2,1)} %reshape.144), calls=%async_computation.1 | async-start | bytes 819200 | tf_op jit(solution)/shard_map/all_to_all | solution.py:88
  110.2 5.7 %copy-start.1 = (bf16[4,8,80,80]{3,2,1,0:T(8,128)(2,1)}, bf16[4,8,80,80]{3,2,1,0:T(8,128)(2,1)S(1)}, u32[]{:S(2)}) copy-start(bf16[4,8,80,80]{3,2,1,0:T(8,128)(2,1)S(1)} %copy.71) | copy-start | bytes 1228804
  126.2 9.8 %copy-start = (f32[3,8,80,80]{2,3,0,1:T(8,128)S(1)}, f32[3,8,80,80]{2,3,0,1:T(8,128)}, u32[]{:S(2)}) copy-start(f32[3,8,80,80]{2,3,0,1:T(8,128)} %get-tuple-element.61) | copy-start | bytes 1843204
Sparse Core Ops, SparseCore 0:
  9.9 47.6 all-gather.2
where the time goes:
time: 193 us; the launch traced here: 192 us
  blocking collectives  53.4 us (28%)
  waiting for transfers between devices  41.2 us (21%)
  matrix products  38.6 us (20%)
  local copies, waits for them, and re-layouts  24 us (12%)
  between operations  14.2 us (7%)
  starting transfers between devices  10.9 us (6%)
  other arithmetic  9.58 us (5%)
    psum x1, blocking collectives, per_device(): lax.psum(jnp.sum(density, axis=1), ('ka', 'op', 'row')) / count_all  41.1 us
    all_gather x1, waiting for transfers between devices, per_device(): lax.all_gather(operators, ('ka', 'row'), axis=1, tiled=True)  35.7 us
    all_gather x1, blocking collectives, per_device(): points = lax.all_gather(kgrid, 'op', axis=1, tiled=True)  12.3 us
    dot_general x4, matrix products, mix_table(): jnp.einsum('kr,nrx->nkx', table, block, preferred_element_type=jnp.float32)  11.1 us
    dot_general x1, matrix products, density_terms(): jnp.einsum('aknm,bkmn->abk', left_real, prod_imag, precision=lax.Precisio...  7.35 us
    dot_general x1, matrix products, density_terms(): jnp.einsum('aknm,bkmn->abk', left_imag, prod_real, precision=lax.Precisio...  6.79 us
    unnamed x2, other arithmetic  6.14 us
    dot_general x4, matrix products, multiply(): jnp.einsum('knm,bkml->bknl', left, right, preferred_element_type=jnp.floa...  5.81 us
  transfers between devices with their start and end apart: 3, of which 2 were waited for; matrix products, arithmetic and copies ran while one was open for 8% of the time, Pallas kernels for 0%

commit v1 on v0

--- a/solution.py
+++ b/solution.py
@@ -1,3 +1,4 @@
+import functools
 import math
 import jax
 import jax.numpy as jnp
@@ -7,6 +8,13 @@
 W = 80
 GRID = 64
 SMEARING = 0.5
+
+
+def work_pipes(incoming_x, mesh_dim, axis_id):
+    return lax.psum(lax.psum(incoming_x, axis_name=mesh_dim), axis_id)
+
+
+wrap_clusters = functools.partial(work_pipes, mesh_dim=("op", "row"), axis_id="ka")
 
 
 def phase_pair(points, lattice, weights):
@@ -117,7 +125,7 @@
         rotate, (real_k.reshape(4, own, W, W), imag_k.reshape(4, own, W, W))
     )
     density = density_terms(rot_real, rot_imag)
-    magnetization = lax.psum(jnp.sum(density, axis=1), ("ka", "op", "row")) / count_all
+    magnetization = wrap_clusters(jnp.sum(density, axis=1)) / count_all
     return (density, magnetization)
 
 

time: 193 us -> 181 us (0.938)
  the two profiles are of different devices: /device:TPU:10 before, /device:TPU:0 now
where the time goes in v1:
time: 181 us; the launch traced here: 180 us
  waiting for transfers between devices  45.9 us (25%)
  blocking collectives  39.2 us (22%)
  matrix products  38.7 us (21%)
  local copies, waits for them, and re-layouts  24 us (13%)
  between operations  14.2 us (8%)
  other arithmetic  9.58 us (5%)
  starting transfers between devices  8.28 us (5%)
    all_gather x1, waiting for transfers between devices, per_device(): lax.all_gather(operators, ('ka', 'row'), axis=1, tiled=True)  35.9 us
    psum x2, blocking collectives, work_pipes(): return lax.psum(lax.psum(incoming_x, axis_name=mesh_dim), axis_id)  25.4 us
    all_gather x1, blocking collectives, per_device(): points = lax.all_gather(kgrid, 'op', axis=1, tiled=True)  13.8 us
    dot_general x4, matrix products, mix_table(): jnp.einsum('kr,nrx->nkx', table, block, preferred_element_type=jnp.float32)  11.1 us
    dot_general x1, matrix products, density_terms(): jnp.einsum('aknm,bkmn->abk', left_real, prod_imag, precision=lax.Precisio...  7.35 us
    all_to_all x1, waiting for transfers between devices, per_device(): lax.all_to_all(imag_k, 'op', split_axis=1, concat_axis=0, tiled=True)  7.15 us
    dot_general x1, matrix products, density_terms(): jnp.einsum('aknm,bkmn->abk', left_imag, prod_real, precision=lax.Precisio...  6.79 us
    unnamed x2, other arithmetic  6.14 us
  transfers between devices with their start and end apart: 3, of which 3 were waited for; matrix products, arithmetic and copies ran while one was open for 9% of the time, Pallas kernels for 0%

profile of v1, /device:TPU:0, one launch (start us, length us, event | category | flops | bytes accessed | tf_op | source)
XLA Modules:
  0.0 180.2 jit_solution(12710832793720054370)
XLA Ops:
  7.9 13.8 %all-gather = s32[4,8,3]{1,2,0:T(4,128)S(1)} all-gather(s32[1,8,3]{1,2,0:T(4,128)} %bitcast.177), channel_id=1, replica_groups=mesh['ka'=4,'op'=4,'row'=2] {'op'}, dimensions={0}, use_global_device_ids=true | all-gather | bytes 480 | tf_op jit(solution)/shard_map/all_gather | solution.py:85
  23.3 35.9 %all-gather.3.cloned.1.call-done = bf16[1,256,12800]{2,1,0:T(8,128)(2,1)} async-done(((bf16[1,32,12800]{2,1,0:T(8,128)(2,1)}), bf16[1,256,12800]{2,1,0:T(8,128)(2,1)}) %all-gather.3.cloned.1.call-update) | async-done | bytes 6553616 | tf_op jit(solution)/shard_map/all_gather | solution.py:90
  59.1 2.8 %fusion.26 = f32[32,6400]{1,0:T(8,128)S(1)} fusion(bf16[1,256,12800]{2,1,0:T(8,128)(2,1)} %all-gather.3.cloned.1.call-done, f32[256]{0:T(256)S(1)} %convert_divide_fusion, s32[256]{0:T(256)S(1)} %bitcast.168, s32[32]{0:T(128)S(1)} %get-tuple-element.69, s32[256]{0:T(256)S(1)} %bitcast.172, s32[32]{0:T(128)S(1)} %get-tuple-element.70, s32[256]{0:T(256)S(1)} %bitcast.164, ...), kind=kOutput, calls=%fused_computation.35 | convolution fusion | flops 105021440 | bytes 4100480 | tf_op jit(solution)/shard_map/kr,nrx->nkx/dot_general | solution.py:35
  61.9 2.8 %fusion.25 = bf16[1,32,6400]{2,1,0:T(8,128)(2,1)S(1)} fusion(f32[32,6400]{1,0:T(8,128)S(1)} %fusion.26, bf16[1,256,12800]{2,1,0:T(8,128)(2,1)} %all-gather.3.cloned.1.call-done, f32[256]{0:T(256)S(1)} %convert_divide_fusion, s32[256]{0:T(256)S(1)} %bitcast.169, s32[32]{0:T(128)S(1)} %get-tuple-element.69, s32[256]{0:T(256)S(1)} %bitcast.173, ...), kind=kOutput, calls=%fused_computation.32 | convolution fusion | flops 105431040 | bytes 4510080 | tf_op jit(solution)/shard_map/kr,nrx->nkx/dot_general | solution.py:35
  65.8 3.1 %reduce.10 = bf16[32,6400]{1,0:T(8,128)(2,1)S(1)} reduce(bf16[32,1,6400]{2,1,0:T(2,128)(2,1)S(1)} %bitcast.162, bf16[]{:T(256)} %broadcast.118), dimensions={1}, to_apply=%bitcast.125.reduce_sub_computation | reduce | bytes 819202
  68.9 0.9 reshape.142
  69.8 4.6 %all-to-all-start = ((bf16[4,2,25600]{2,1,0:T(2,128)(2,1)}), bf16[4,2,25600]{2,1,0:T(2,128)(2,1)S(1)}, u32[]{:S(2)}, u32[]{:S(2)}) async-start(bf16[4,2,25600]{2,1,0:T(2,128)(2,1)} %reshape.142), calls=%async_computation | async-start | bytes 819200 | tf_op jit(solution)/shard_map/all_to_all | solution.py:95
  74.4 2.8 %fusion.27 = f32[32,6400]{1,0:T(8,128)S(1)} fusion(bf16[1,256,12800]{2,1,0:T(8,128)(2,1)} %all-gather.3.cloned.1.call-done, f32[256]{0:T(256)S(1)} %convert_divide_fusion, s32[256]{0:T(256)S(1)} %bitcast.170, s32[32]{0:T(128)S(1)} %get-tuple-element.69, s32[256]{0:T(256)S(1)} %bitcast.174, s32[32]{0:T(128)S(1)} %get-tuple-element.70, s32[256]{0:T(256)S(1)} %bitcast.166, ...), kind=kOutput, calls=%fused_computation.36 | convolution fusion | flops 105021440 | bytes 4100480 | tf_op jit(solution)/shard_map/kr,nrx->nkx/dot_general | solution.py:35
  77.2 2.8 %fusion.24 = bf16[1,32,6400]{2,1,0:T(8,128)(2,1)S(1)} fusion(f32[32,6400]{1,0:T(8,128)S(1)} %fusion.27, bf16[1,256,12800]{2,1,0:T(8,128)(2,1)} %all-gather.3.cloned.1.call-done, f32[256]{0:T(256)S(1)} %convert_divide_fusion, s32[256]{0:T(256)S(1)} %bitcast.171, s32[32]{0:T(128)S(1)} %get-tuple-element.69, s32[256]{0:T(256)S(1)} %bitcast.175, ...), kind=kOutput, calls=%fused_computation.31 | convolution fusion | flops 105431040 | bytes 4510080 | tf_op jit(solution)/shard_map/kr,nrx->nkx/dot_general | solution.py:35
  80.6 3.1 %reduce.11 = bf16[32,6400]{1,0:T(8,128)(2,1)S(1)} reduce(bf16[32,1,6400]{2,1,0:T(2,128)(2,1)S(1)} %bitcast.163, bf16[]{:T(256)} %broadcast.118), dimensions={1}, to_apply=%bitcast.124.reduce_sub_computation | reduce | bytes 819202
  83.7 0.9 reshape.144
  84.6 2.3 %all-to-all-done = bf16[4,2,25600]{2,1,0:T(2,128)(2,1)S(1)} async-done(((bf16[4,2,25600]{2,1,0:T(2,128)(2,1)}), bf16[4,2,25600]{2,1,0:T(2,128)(2,1)S(1)}, u32[]{:S(2)}, u32[]{:S(2)}) %all-to-all-start) | async-done | bytes 409632 | tf_op jit(solution)/shard_map/all_to_all | solution.py:95
  86.8 3.6 %all-to-all-start.1 = ((bf16[4,2,25600]{2,1,0:T(2,128)(2,1)}), bf16[4,2,25600]{2,1,0:T(2,128)(2,1)S(1)}, u32[]{:S(2)}, u32[]{:S(2)}) async-start(bf16[4,2,25600]{2,1,0:T(2,128)(2,1)} %reshape.144), calls=%async_computation.1 | async-start | bytes 819200 | tf_op jit(solution)/shard_map/all_to_all | solution.py:96
  91.4 2.3 %bitcast_reduce_fusion.1 = bf16[32,6400]{1,0:T(8,128)(2,1)S(1)} fusion(bf16[32,1,6400]{2,1,0:T(2,128)(2,1)S(1)} %reshape.143), kind=kLoop, calls=%fused_computation.108 | loop fusion | bytes 819200 | tf_op jit(solution)/shard_map/all_to_all | solution.py:95
  93.6 1.1 reshape.122
  94.7 7.1 %all-to-all-done.1 = bf16[4,2,25600]{2,1,0:T(2,128)(2,1)S(1)} async-done(((bf16[4,2,25600]{2,1,0:T(2,128)(2,1)}), bf16[4,2,25600]{2,1,0:T(2,128)(2,1)S(1)}, u32[]{:S(2)}, u32[]{:S(2)}) %all-to-all-start.1) | async-done | bytes 409632 | tf_op jit(solution)/shard_map/all_to_all | solution.py:96
  102.2 2.3 %bitcast_reduce_fusion = bf16[32,6400]{1,0:T(8,128)(2,1)S(1)} fusion(bf16[32,1,6400]{2,1,0:T(2,128)(2,1)S(1)} %reshape.145), kind=kLoop, calls=%fused_computation.107 | loop fusion | bytes 819200 | tf_op jit(solution)/shard_map/all_to_all | solution.py:96
  104.5 1.1 reshape.124
  105.6 7.9 %while.12 = (s32[]{:T(128)}, bf16[4,8,80,80]{2,3,1,0:T(8,128)(2,1)S(1)}, bf16[4,8,80,80]{2,3,1,0:T(8,128)(2,1)S(1)}, bf16[4,8,80,80]{3,2,1,0:T(8,128)(2,1)S(1)},...) while((s32[]{:T(128)}, ...), condition=%wide.region_1.2_spmd, body=%wide.region_0.1_spmd.sunk | while | flops 65945600 | bytes 5038189 | solution.py:124
  114.2 1.6 copy.74
  115.7 3.7 %gather_fusion = bf16[80,8]{1,0:T(8,128)(2,1)S(1)} fusion(bf16[8,80,80]{0,2,1:T(8,128)(2,1)} %copy.74, s32[80]{0:T(128)S(1)} %or_bitcast_fusion), kind=kCustom, calls=%fused_computation | custom fusion | bytes 3200 | tf_op jit(solution)/shard_map/jit(diagonal)/gather | solution.py:57
  119.6 1.1 copy.73
  120.7 1.2 fusion.48
  121.9 2.2 %fusion.28 = f32[3,8,80,80]{2,3,0,1:T(8,128)} fusion(f32[8,3,80,80]{3,2,1,0:T(8,128)S(1)} %fusion.46, bf16[4,8,80,80]{3,2,1,0:T(8,128)(2,1)} %copy.73, bf16[4,8,80,80]{2,3,1,0:T(8,128)(2,1)S(1)} %get-tuple-element.40), kind=kOutput, calls=%fused_computation.38 | convolution fusion | flops 24729600 | bytes 1802240 | tf_op jit(solution)/shard_map/knm,bkml->bknl/dot_general | solution.py:62
  124.1 2.4 %copy.78 = f32[3,8,80,80]{3,0,2,1:T(4,128)} copy(f32[3,8,80,80]{2,3,0,1:T(8,128)} %fusion.28) | data formatting | bytes 1228800 | tf_op jit(solution)/shard_map/sub | solution.py:64
  126.6 1.1 convert_multiply_fusion
  127.7 2.1 %fusion.29 = f32[3,8,80,80]{2,3,0,1:T(8,128)} fusion(f32[8,3,80,80]{3,2,1,0:T(8,128)S(1)} %fusion.48, bf16[4,8,80,80]{3,2,1,0:T(8,128)(2,1)} %copy.73, bf16[4,8,80,80]{2,3,1,0:T(8,128)(2,1)S(1)} %get-tuple-element.41), kind=kOutput, calls=%fused_computation.40 | convolution fusion | flops 24729600 | bytes 1802240 | tf_op jit(solution)/shard_map/knm,bkml->bknl/dot_general | solution.py:62
  129.9 2.4 %copy.76 = f32[3,8,80,80]{3,0,2,1:T(4,128)} copy(f32[3,8,80,80]{2,3,0,1:T(8,128)} %fusion.29) | data formatting | bytes 1228800 | tf_op jit(solution)/shard_map/add | solution.py:65
  132.3 7.4 %fusion.34 = f32[8,3,3]{2,1,0:T(4,128)S(1)} fusion(f32[3,8,80,80]{3,0,2,1:T(4,128)} %copy.76, f32[3,8,80,80]{2,3,0,1:T(8,128)S(1)} %get-tuple-element.62), kind=kOutput, calls=%fused_computation.45 | convolution fusion | flops 5529600 | bytes 1229088 | tf_op jit(solution)/shard_map/aknm,bkmn->abk/dot_general | solution.py:69
  139.7 6.8 %fusion.43 = f32[3,3,8]{0,1,2:T(4,128)S(1)} fusion(f32[8,3,3]{2,1,0:T(4,128)S(1)} %fusion.34, f32[3,8,80,80]{3,0,2,1:T(4,128)} %copy.78, f32[3,8,80,80]{2,3,0,1:T(8,128)S(1)} %copy-done), kind=kOutput, calls=%fused_computation.48 | convolution fusion | flops 5529672 | bytes 1229376 | tf_op jit(solution)/shard_map/aknm,bkmn->abk/dot_general | solution.py:71
  147.4 19.5 %psum.14 = f32[3]{0:T(128)S(1)} all-reduce(f32[3]{0:T(128)S(1)} %get-tuple-element.59), channel_id=1, replica_groups=mesh['ka'=4,'op'=4,'row'=2] {'op','row'}, use_global_device_ids=true, to_apply=%region_3.4 | all-reduce | flops 3 | bytes 24 | tf_op jit(solution)/shard_map/psum | solution.py:14
  166.8 6.0 %psum.15 = f32[3]{0:T(128)S(1)} all-reduce(f32[3]{0:T(128)S(1)} %psum.14), channel_id=1, replica_groups=mesh['ka'=4,'op'=4,'row'=2] {'ka'}, use_global_device_ids=true, to_apply=%region_4.5 | all-reduce | flops 3 | bytes 24 | tf_op jit(solution)/shard_map/psum | solution.py:14
  (65 shorter events, 15.2 us)
Async XLA Ops:
  7.2 51.9 %all-gather.3.cloned.1.call-start = ((), (), s32[]{:S(2)}) async-start(), calls=%async_computation.2 | async-start | bytes 7372800 | tf_op jit(solution)/shard_map/all_gather | solution.py:90
  69.8 17.0 %all-to-all-start = ((bf16[4,2,25600]{2,1,0:T(2,128)(2,1)}), bf16[4,2,25600]{2,1,0:T(2,128)(2,1)S(1)}, u32[]{:S(2)}, u32[]{:S(2)}) async-start(bf16[4,2,25600]{2,1,0:T(2,128)(2,1)} %reshape.142), calls=%async_computation | async-start | bytes 819200 | tf_op jit(solution)/shard_map/all_to_all | solution.py:95
  77.2 13.4 %copy-start.2 = (bf16[8,12800]{1,0:T(8,128)(2,1)S(1)}, bf16[8,12800]{1,0:T(8,128)(2,1)}, u32[]{:S(2)}) copy-start(bf16[8,12800]{1,0:T(8,128)(2,1)} %param.11) | copy-start | bytes 614404
  86.8 15.0 %all-to-all-start.1 = ((bf16[4,2,25600]{2,1,0:T(2,128)(2,1)}), bf16[4,2,25600]{2,1,0:T(2,128)(2,1)S(1)}, u32[]{:S(2)}, u32[]{:S(2)}) async-start(bf16[4,2,25600]{2,1,0:T(2,128)(2,1)} %reshape.144), calls=%async_computation.1 | async-start | bytes 819200 | tf_op jit(solution)/shard_map/all_to_all | solution.py:96
  113.8 5.7 %copy-start.1 = (bf16[4,8,80,80]{3,2,1,0:T(8,128)(2,1)}, bf16[4,8,80,80]{3,2,1,0:T(8,128)(2,1)S(1)}, u32[]{:S(2)}) copy-start(bf16[4,8,80,80]{3,2,1,0:T(8,128)(2,1)S(1)} %copy.71) | copy-start | bytes 1228804
  129.9 9.8 %copy-start = (f32[3,8,80,80]{2,3,0,1:T(8,128)S(1)}, f32[3,8,80,80]{2,3,0,1:T(8,128)}, u32[]{:S(2)}) copy-start(f32[3,8,80,80]{2,3,0,1:T(8,128)} %get-tuple-element.61) | copy-start | bytes 1843204
Sparse Core Ops, SparseCore 0:
  9.9 49.2 all-gather.2
